TPU v7x, 512 devices: a whole 4x8x8 slice. The times are simulated.
512 devices in a mesh: expert: 32 (over z, y_hi), tensor: 16 (over y_lo, x, core).
Axes of the slice: x: 4, y: 8 (y_hi: 4, y_lo: 2; y = y_hi * 2 + y_lo), z: 8, core: 2. Of those that a mesh axis runs over, the one named last changes fastest.
Arguments:
- tokens: bfloat16 [4096, 3072], P('expert', 'tensor'), may hold values from -6 to 6
- expert_ids: int32 [4096, 2], P('expert'), may hold values from 0 to 7, all different within a row; in each aligned block of 128 rows (0 to 127, 128 to 255, ...) at most 48 rows name the same one
- joined_weight: bfloat16 [32, 3072, 2, 4096], P('expert', 'tensor'), may hold values from -0.109375 to 0.109375
Outputs:
- hidden: bfloat16 [4096, 2, 4, 4096], P('expert', None, None, 'tensor')
Inputs may be any that keep to these rules, and one draw needn't show every extreme that they name: `expert_ids`: each row names 2 different experts. Among the rows of one device (each aligned block of 128 rows) no expert is named by more than 48 rows, and in some blocks one expert is named by exactly 48 rows.
All inputs are finite; a program needn't handle non-finite values.
Results may differ from a plain program's by a relative error of at most 0.001.
Values may be sent and summed in bfloat16 or wider, within the bound.
No kernel may reach another device: no remote copies, remote signals or barrier semaphores. Data moves between devices by JAX's collectives and lax.ppermute only.
A program may use at most 128 MiB of HBM per device.

v0:
```python
import jax
import jax.numpy as jnp
from jax import lax
from jax.sharding import PartitionSpec as P

E = 8
TOP = 2
CAP = 48


def activate(gate_up, half_width):
    gate = gate_up[:, :half_width]
    upward = gate_up[:, half_width:]
    return (jax.nn.silu(gate) * upward).astype(jnp.bfloat16)


def give_back(active):
    return lax.all_to_all(active, "expert", split_axis=0, concat_axis=0, tiled=True)


def local(tokens, expert_ids, joined_weight):
    groups = lax.axis_size("tensor")
    blocks = lax.axis_size("expert")
    copies = blocks // E
    local_rows = joined_weight.shape[1]
    half_width = joined_weight.shape[3] // groups
    pieces = joined_weight[0].reshape(local_rows, 2, groups, half_width)
    arranged = lax.all_to_all(pieces, "tensor", split_axis=2, concat_axis=0, tiled=True)
    weights = arranged.reshape(local_rows * groups, 2 * half_width)
    tok_count = tokens.shape[0]
    flat_ids = expert_ids.reshape(-1)
    chosen = (flat_ids[:, None] == jnp.arange(E, dtype=jnp.int32)[None, :]).astype(jnp.int32)
    earlier = jnp.cumsum(chosen, axis=0) - chosen
    position = jnp.sum(earlier * chosen, axis=1)
    slot_index = flat_ids * CAP + position
    pick_table = (slot_index[:, None] == jnp.arange(E * CAP, dtype=jnp.int32)[None, :]).astype(
        jnp.bfloat16
    )
    token_table = pick_table.reshape(tok_count, TOP, E * CAP).sum(axis=1)
    width = tokens.shape[1]
    placed = lax.dot_general(
        token_table, tokens, (((0,), (0,)), ((), ())), preferred_element_type=jnp.float32
    )
    placed = placed.astype(jnp.bfloat16).reshape(E, 1, CAP, width)
    outgoing = jnp.broadcast_to(placed, (E, copies, CAP, width)).reshape(blocks, CAP, width)
    received = lax.all_to_all(outgoing, "expert", split_axis=0, concat_axis=0, tiled=True)
    slot_count = received.shape[1]
    piece = lax.all_gather(received, "tensor", axis=2, tiled=True)
    row_block = piece.reshape(blocks * slot_count, piece.shape[2])
    gate_up = jnp.dot(row_block, weights, preferred_element_type=jnp.float32)
    returned = give_back(activate(gate_up, half_width).reshape(blocks, slot_count, half_width))
    grouped = (
        returned.reshape(E, copies, CAP, half_width)
        .transpose(0, 2, 1, 3)
        .reshape(E * CAP, copies * half_width)
    )
    hidden = jnp.dot(pick_table, grouped, preferred_element_type=jnp.float32).astype(jnp.bfloat16)
    return hidden.reshape(tok_count, TOP, copies, half_width)


def solution(mesh):
    placed = (P("expert", "tensor"), P("expert", None), P("expert", "tensor", None, None))
    return jax.shard_map(
        local,
        mesh=mesh,
        in_specs=placed,
        out_specs=P("expert", None, None, "tensor"),
        check_vma=False,
    )
```

profile of v0, /device:TPU:10, one launch (start us, length us, event | category | flops | bytes accessed | tf_op | source)
XLA Modules:
  0.0 299.9 jit_solution(4116273108823073041)
XLA Ops:
  6.5 0.0 all-gather.2.cloned.1.call-start
  6.5 0.8 copy.55
  7.3 0.1 reshape.62
  7.5 0.1 eq.46
  7.6 0.6 reduce-window.6
  8.2 0.2 slice_reduce_fusion
  8.5 0.1 fusion.5
  8.6 0.1 reduce_sum.24
  8.7 0.1 copy.57
  8.8 0.7 multiply_add_fusion
  9.5 0.1 fusion.2
  9.6 0.0 copy-done
  9.6 0.2 convolution_convert_fusion.1
  9.8 0.1 copy.58
  9.9 0.1 broadcast_in_dim.5
  10.0 37.4 %all_to_all.25 = bf16[32,48,192]{2,1,0:T(8,128)(2,1)S(1)} all-to-all(bf16[32,48,192]{2,1,0:T(8,128)(2,1)S(1)} %bitcast.36), channel_id=1, replica_groups=mesh['expert'=32,'tensor'=16] {'expert'}, dimensions={0} | all-to-all | bytes 1179648 | tf_op jit(solution)/shard_map/all_to_all | solution.py:46
  47.4 2.3 copy.59
  49.7 0.0 all-gather.2.cloned.1.call-update
  49.7 4.6 %reshape_squeeze.3 = bf16[192,2,16,256]{3,2,1,0:T(8,128)(2,1)S(1)} reshape(bf16[1,192,2,4096]{3,2,1,0:T(2,128)(2,1)} %param.5) | data formatting | bytes 6291456 | tf_op jit(solution)/shard_map/reshape;squeeze | solution.py:27
  54.3 3.0 %copy.61 = bf16[192,2,16,256]{3,1,0,2:T(2,128)(2,1)S(1)} copy(bf16[192,2,16,256]{3,2,1,0:T(8,128)(2,1)S(1)} %reshape_squeeze.3) | data formatting | bytes 6291456 | tf_op jit(solution)/shard_map/reshape;squeeze | solution.py:27
  57.3 75.2 %all_to_all.26 = bf16[192,2,16,256]{3,1,0,2:T(2,128)(2,1)S(1)} all-to-all(bf16[192,2,16,256]{3,1,0,2:T(2,128)(2,1)S(1)} %copy.61), channel_id=1, replica_groups=mesh['expert'=32,'tensor'=16] {'tensor'}, dimensions={2} | all-to-all | bytes 6291456 | tf_op jit(solution)/shard_map/all_to_all | solution.py:28
  132.5 0.5 copy.63
  133.1 86.2 %all-gather.2.cloned.1.call-done = bf16[32,48,3072]{1,0,2:T(8,128)(2,1)} async-done(((bf16[32,48,192]{1,0,2:T(8,128)(2,1)}), bf16[32,48,3072]{1,0,2:T(8,128)(2,1)}) %all-gather.2.cloned.1.call-update) | async-done | bytes 9437200 | tf_op jit(solution)/shard_map/all_gather | solution.py:48
  219.3 26.3 %copy.60 = bf16[32,48,3072]{2,1,0:T(8,128)(2,1)} copy(bf16[32,48,3072]{1,0,2:T(8,128)(2,1)} %all-gather.2.cloned.1.call-done) | data formatting | bytes 18874368 | tf_op jit(solution)/shard_map/all_gather | solution.py:48
  245.5 7.5 %fusion.7 = f32[1536,512]{1,0:T(8,128)S(1)} fusion(bf16[1536,3072]{1,0:T(8,128)(2,1)} %bitcast.31, bf16[3072,512]{1,0:T(8,128)(2,1)S(1)} %bitcast.32), kind=kOutput, calls=%fused_computation.18 | convolution fusion | flops 4831838208 | bytes 15728640 | tf_op jit(solution)/shard_map/dot_general | solution.py:50
  253.1 1.3 fusion
  254.4 9.7 %all-to-all-start.2 = ((bf16[32,48,256]{2,1,0:T(8,128)(2,1)}), bf16[32,48,256]{2,1,0:T(8,128)(2,1)S(1)}, u32[]{:S(2)}, u32[]{:S(2)}) async-start(bf16[32,48,256]{2,1,0:T(8,128)(2,1)} %bitcast.7), calls=%async_computation.2 | async-start | bytes 1572864 | tf_op jit(solution)/shard_map/all_to_all | solution.py:18
  264.1 26.8 %all-to-all-done.2 = bf16[32,48,256]{2,1,0:T(8,128)(2,1)S(1)} async-done(((bf16[32,48,256]{2,1,0:T(8,128)(2,1)}), bf16[32,48,256]{2,1,0:T(8,128)(2,1)S(1)}, u32[]{:S(2)}, u32[]{:S(2)}) %all-to-all-start.2) | async-done | bytes 786464 | tf_op jit(solution)/shard_map/all_to_all | solution.py:18
  290.8 0.4 copy.62
  291.3 0.2 copy.64
  291.4 0.5 convolution_convert_fusion
  291.9 1.2 reshape.70
  (5 shorter events, 0.1 us)
Async XLA Ops:
  6.5 3.1 %copy-start = (bf16[128,192]{0,1:T(8,128)(2,1)S(1)}, bf16[128,192]{0,1:T(8,128)(2,1)}, u32[]{:S(2)}) copy-start(bf16[128,192]{0,1:T(8,128)(2,1)} %param.3) | copy-start | bytes 147460
  6.5 212.7 %all-gather.2.cloned.1.call-start = ((), (), s32[]{:S(2)}) async-start(), calls=%async_computation.3 | async-start | bytes 26738688 | tf_op jit(solution)/shard_map/all_gather | solution.py:48
  254.4 36.5 %all-to-all-start.2 = ((bf16[32,48,256]{2,1,0:T(8,128)(2,1)}), bf16[32,48,256]{2,1,0:T(8,128)(2,1)S(1)}, u32[]{:S(2)}, u32[]{:S(2)}) async-start(bf16[32,48,256]{2,1,0:T(8,128)(2,1)} %bitcast.7), calls=%async_computation.2 | async-start | bytes 1572864 | tf_op jit(solution)/shard_map/all_to_all | solution.py:18
Sparse Core Ops, SparseCore 0:
  49.8 169.3 all-gather.1
where the time goes:
time: 301 us; the launch traced here: 300 us
  blocking collectives  113 us (38%)
  waiting for transfers between devices  113 us (38%)
  local copies, waits for them, and re-layouts  40.1 us (13%)
  between operations  13.5 us (4%)
  starting transfers between devices  9.68 us (3%)
  matrix products  8.2 us (3%)
    all_gather x1, waiting for transfers between devices, local(): piece = lax.all_gather(received, 'tensor', axis=2, tiled=True)  86.2 us
    all_to_all x1, blocking collectives, local(): lax.all_to_all(pieces, 'tensor', split_axis=2, concat_axis=0, tiled=True)  75.2 us
    all_to_all x1, blocking collectives, local(): lax.all_to_all(outgoing, 'expert', split_axis=0, concat_axis=0, tiled=True)  37.4 us
    all_to_all x1, waiting for transfers between devices, give_back(): lax.all_to_all(active, 'expert', split_axis=0, concat_axis=0, tiled=True)  26.8 us
    all_gather x1, local copies, waits for them, and re-layouts, local(): piece = lax.all_gather(received, 'tensor', axis=2, tiled=True)  26.3 us
    all_to_all x1, starting transfers between devices, give_back(): lax.all_to_all(active, 'expert', split_axis=0, concat_axis=0, tiled=True)  9.68 us
    another operation x2, local copies, waits for them, and re-layouts, local(): pieces = joined_weight[0].reshape(local_rows, 2, groups, half_width)  7.59 us
    dot_general x1, matrix products, local(): gate_up = jnp.dot(row_block, weights, preferred_element_type=jnp.float32)  7.53 us
  transfers between devices with their start and end apart: 2, of which 2 were waited for; matrix products, arithmetic and copies ran while one was open for 3% of the time, Pallas kernels for 0%

commit v1 on v0

--- a/solution.py
+++ b/solution.py
@@ -45,7 +45,9 @@
     outgoing = jnp.broadcast_to(placed, (E, copies, CAP, width)).reshape(blocks, CAP, width)
     received = lax.all_to_all(outgoing, "expert", split_axis=0, concat_axis=0, tiled=True)
     slot_count = received.shape[1]
-    piece = lax.all_gather(received, "tensor", axis=2, tiled=True)
+    piece = jnp.concatenate(
+        lax.all_to_all(jnp.stack([received] * lax.axis_size("tensor")), "tensor", 0, 0), axis=2
+    )
     row_block = piece.reshape(blocks * slot_count, piece.shape[2])
     gate_up = jnp.dot(row_block, weights, preferred_element_type=jnp.float32)
     returned = give_back(activate(gate_up, half_width).reshape(blocks, slot_count, half_width))

time: 301 us -> 376 us (1.25)
  the two profiles are of different devices: /device:TPU:10 before, /device:TPU:14 now
where the time goes in v1:
time: 376 us; the launch traced here: 375 us
  waiting for transfers between devices  232 us (62%)
  local copies, waits for them, and re-layouts  57 us (15%)
  blocking collectives  45 us (12%)
  starting transfers between devices  29.3 us (8%)
  matrix products  8.22 us (2%)
    all_to_all x1, waiting for transfers between devices, local(): lax.all_to_all(jnp.stack([received] * lax.axis_size('tensor')), 'tensor',...  192 us
    all_to_all x1, blocking collectives, local(): lax.all_to_all(pieces, 'tensor', split_axis=2, concat_axis=0, tiled=True)  45 us
    all_to_all x1, waiting for transfers between devices, give_back(): lax.all_to_all(active, 'expert', split_axis=0, concat_axis=0, tiled=True)  26.8 us
    another operation x1, local copies, waits for them, and re-layouts, local(): row_block = piece.reshape(blocks * slot_count, piece.shape[2])  20.4 us
    all_to_all x1, starting transfers between devices, local(): lax.all_to_all(outgoing, 'expert', split_axis=0, concat_axis=0, tiled=True)  15.2 us
    reshape x1, local copies, waits for them, and re-layouts, local(): jnp.concatenate(lax.all_to_all(jnp.stack([received] * lax.axis_size('tens...  14.1 us
    all_to_all x1, waiting for transfers between devices, local(): lax.all_to_all(outgoing, 'expert', split_axis=0, concat_axis=0, tiled=True)  13.4 us
    another operation x2, local copies, waits for them, and re-layouts, local(): pieces = joined_weight[0].reshape(local_rows, 2, groups, half_width)  9.07 us
  transfers between devices with their start and end apart: 3, of which 3 were waited for; matrix products, arithmetic and copies ran while one was open for 3% of the time, Pallas kernels for 0%

profile of v1, /device:TPU:14, one launch (start us, length us, event | category | flops | bytes accessed | tf_op | source)
XLA Modules:
  0.0 374.8 jit_solution(14164862038640929089)
XLA Ops:
  0.0 0.8 copy.36
  0.8 0.1 eq.46
  0.9 0.1 reshape.64
  1.1 0.6 reduce-window.6
  1.7 0.2 slice_reduce_fusion
  1.9 0.1 fusion.5
  2.0 0.1 reduce_sum.24
  2.2 0.1 copy.38
  2.2 0.7 multiply_add_fusion
  2.9 0.1 fusion.2
  3.1 0.2 convolution_convert_fusion.1
  3.3 0.1 copy.39
  3.4 0.9 broadcast_in_dim.5
  4.3 15.2 %all-to-all-start = ((bf16[32,48,192]{2,1,0:T(8,128)(2,1)}), bf16[32,48,192]{2,1,0:T(8,128)(2,1)}, u32[]{:S(2)}, u32[]{:S(2)}) async-start(bf16[32,48,192]{2,1,0:T(8,128)(2,1)} %bitcast.3), calls=%async_computation | async-start | bytes 1572864 | tf_op jit(solution)/shard_map/all_to_all | solution.py:46
  19.5 4.6 %reshape_squeeze.3 = bf16[192,2,16,256]{3,2,1,0:T(8,128)(2,1)S(1)} reshape(bf16[1,192,2,4096]{3,2,1,0:T(2,128)(2,1)} %param.5) | data formatting | bytes 6291456 | tf_op jit(solution)/shard_map/reshape;squeeze | solution.py:27
  24.1 4.5 %copy.41 = bf16[192,2,16,256]{3,1,0,2:T(2,128)(2,1)} copy(bf16[192,2,16,256]{3,2,1,0:T(8,128)(2,1)S(1)} %reshape_squeeze.3) | data formatting | bytes 6291456 | tf_op jit(solution)/shard_map/reshape;squeeze | solution.py:27
  28.6 13.4 %all-to-all-done = bf16[32,48,192]{2,1,0:T(8,128)(2,1)} async-done(((bf16[32,48,192]{2,1,0:T(8,128)(2,1)}), bf16[32,48,192]{2,1,0:T(8,128)(2,1)}, u32[]{:S(2)}, u32[]{:S(2)}) %all-to-all-start) | async-done | bytes 589856 | tf_op jit(solution)/shard_map/all_to_all | solution.py:46
  42.0 45.0 %all_to_all.30 = bf16[192,2,16,256]{3,1,0,2:T(2,128)(2,1)S(1)} all-to-all(bf16[192,2,16,256]{3,1,0,2:T(2,128)(2,1)} %copy.41), channel_id=1, replica_groups=mesh['expert'=32,'tensor'=16] {'tensor'}, dimensions={2} | all-to-all | bytes 6291456 | tf_op jit(solution)/shard_map/all_to_all | solution.py:28
  87.0 6.8 %stack.2 = bf16[16,32,48,192]{3,2,1,0:T(8,128)(2,1)} broadcast(bf16[32,48,192]{2,1,0:T(8,128)(2,1)} %all-to-all-done), dimensions={1,2,3} | broadcast | bytes 10027008 | tf_op jit(solution)/shard_map/stack | solution.py:49
  93.8 7.7 %all-to-all-start.1 = ((bf16[16,32,48,192]{3,2,1,0:T(8,128)(2,1)}), bf16[16,32,48,192]{3,2,1,0:T(8,128)(2,1)}, u32[]{:S(2)}, u32[]{:S(2)}) async-start(bf16[16,32,48,192]{3,2,1,0:T(8,128)(2,1)} %stack.2), calls=%async_computation.1 | async-start | bytes 25165824 | tf_op jit(solution)/shard_map/all_to_all | solution.py:49
  101.6 2.3 copy.43
  103.9 192.0 %all-to-all-done.1 = bf16[16,32,48,192]{3,2,1,0:T(8,128)(2,1)} async-done(((bf16[16,32,48,192]{3,2,1,0:T(8,128)(2,1)}), bf16[16,32,48,192]{3,2,1,0:T(8,128)(2,1)}, u32[]{:S(2)}, u32[]{:S(2)}) %all-to-all-start.1) | async-done | bytes 9437216 | tf_op jit(solution)/shard_map/all_to_all | solution.py:49
  295.9 14.1 %copy.40 = bf16[32,48,16,192]{3,2,1,0:T(8,128)(2,1)} copy(bf16[32,48,16,192]{3,1,0,2:T(8,128)(2,1)} %bitcast.4) | data formatting | bytes 18874368 | tf_op jit(solution)/shard_map/reshape | solution.py:48
  310.0 20.4 %reshape_reshape.3 = bf16[1536,3072]{1,0:T(8,128)(2,1)} reshape(bf16[32,48,16,192]{3,2,1,0:T(8,128)(2,1)} %copy.40) | data formatting | bytes 18874368 | tf_op jit(solution)/shard_map/reshape;reshape | solution.py:51
  330.3 7.5 %fusion.7 = f32[1536,512]{1,0:T(8,128)S(1)} fusion(bf16[1536,3072]{1,0:T(8,128)(2,1)} %reshape_reshape.3, bf16[3072,512]{1,0:T(8,128)(2,1)S(1)} %bitcast.33), kind=kOutput, calls=%fused_computation.18 | convolution fusion | flops 4831838208 | bytes 15728640 | tf_op jit(solution)/shard_map/dot_general | solution.py:52
  337.9 1.3 fusion
  339.2 6.4 %all-to-all-start.3 = ((bf16[32,48,256]{2,1,0:T(8,128)(2,1)}), bf16[32,48,256]{2,1,0:T(8,128)(2,1)S(1)}, u32[]{:S(2)}, u32[]{:S(2)}) async-start(bf16[32,48,256]{2,1,0:T(8,128)(2,1)} %bitcast.7), calls=%async_computation.3 | async-start | bytes 1572864 | tf_op jit(solution)/shard_map/all_to_all | solution.py:18
  345.7 26.8 %all-to-all-done.3 = bf16[32,48,256]{2,1,0:T(8,128)(2,1)S(1)} async-done(((bf16[32,48,256]{2,1,0:T(8,128)(2,1)}), bf16[32,48,256]{2,1,0:T(8,128)(2,1)S(1)}, u32[]{:S(2)}, u32[]{:S(2)}) %all-to-all-start.3) | async-done | bytes 786464 | tf_op jit(solution)/shard_map/all_to_all | solution.py:18
  372.5 0.4 copy.42
  373.0 0.2 copy.44
  373.1 0.5 convolution_convert_fusion
  373.6 1.2 reshape.72
  (10 shorter events, 0.1 us)
Async XLA Ops:
  0.0 3.1 copy-start
  4.3 37.7 %all-to-all-start = ((bf16[32,48,192]{2,1,0:T(8,128)(2,1)}), bf16[32,48,192]{2,1,0:T(8,128)(2,1)}, u32[]{:S(2)}, u32[]{:S(2)}) async-start(bf16[32,48,192]{2,1,0:T(8,128)(2,1)} %bitcast.3), calls=%async_computation | async-start | bytes 1572864 | tf_op jit(solution)/shard_map/all_to_all | solution.py:46
  93.8 202.0 %all-to-all-start.1 = ((bf16[16,32,48,192]{3,2,1,0:T(8,128)(2,1)}), bf16[16,32,48,192]{3,2,1,0:T(8,128)(2,1)}, u32[]{:S(2)}, u32[]{:S(2)}) async-start(bf16[16,32,48,192]{3,2,1,0:T(8,128)(2,1)} %stack.2), calls=%async_computation.1 | async-start | bytes 25165824 | tf_op jit(solution)/shard_map/all_to_all | solution.py:49
  310.0 20.4 %copy-start.2 = (bf16[384,8,2,256]{3,1,2,0:T(8,128)(2,1)S(1)}, bf16[384,8,2,256]{3,1,2,0:T(8,128)(2,1)}, u32[]{:S(2)}) copy-start(bf16[384,8,2,256]{3,1,2,0:T(8,128)(2,1)} %copy.43) | copy-start | bytes 9437188
  339.2 33.3 %all-to-all-start.3 = ((bf16[32,48,256]{2,1,0:T(8,128)(2,1)}), bf16[32,48,256]{2,1,0:T(8,128)(2,1)S(1)}, u32[]{:S(2)}, u32[]{:S(2)}) async-start(bf16[32,48,256]{2,1,0:T(8,128)(2,1)} %bitcast.7), calls=%async_computation.3 | async-start | bytes 1572864 | tf_op jit(solution)/shard_map/all_to_all | solution.py:18
  345.7 29.1 %copy-start.1 = (bf16[128,192]{0,1:T(8,128)(2,1)S(1)}, bf16[128,192]{0,1:T(8,128)(2,1)}, u32[]{:S(2)}) copy-start(bf16[128,192]{0,1:T(8,128)(2,1)} %param.3) | copy-start | bytes 147460
